TPU v7x, 512 devices: a 8x2x16 block of a 8x8x16 slice. The times are simulated.
512 devices in a mesh: beam: 2 (over y), tm: 16 (over z), sect: 8 (over x), pol: 2 (over core).
Axes of the slice: x: 8, y: 2, z: 16, core: 2. Of those that a mesh axis runs over, the one named last changes fastest.
The devices are a block of a 8x8x16 slice.
Arguments:
- signal: float32 [2, 2, 8192, 4096], P(None, 'pol', ('beam', 'tm', 'sect')), parts along dimension 2, may hold values from -6 to 6
- coarse_taps: float32 [16, 4096], replicated, may hold values from -1.5 to 1.5
- fine_taps: float32 [16, 1024], replicated, may hold values from -1.5 to 1.5
- channel_order: int32 [4096], replicated, may hold values from 0 to 4095, each once
Outputs:
- fine_spectra: float32 [2, 2, 8192, 4, 1024], P(None, 'pol', ('beam', 'tm', 'sect')), parts along dimension 2
There are 2 independent parts, one for each index of `beam`. A program takes and returns all parts, laid end to end along the dimension named above; an argument that names none is the same for every part. Nothing has to cross between parts.
Inputs may be any that keep to these rules, and one draw needn't show every extreme that they name: `channel_order`: each of the 4096 coarse channels appears exactly once.
All inputs are finite; a program needn't handle non-finite values.
Results may differ from a plain program's by a relative error of at most 0.0001.
Values sent between devices are 32-bit elements; how exact they have to be, the bound alone decides.
A program may use at most 64 MiB of HBM per device.

v0:
```python
from functools import partial
import math

import jax
import jax.numpy as jnp
from jax import lax
from jax.experimental import pallas as pl
from jax.experimental.pallas import tpu as pltpu
from jax.sharding import PartitionSpec as P
import ml_dtypes
import numpy as np

LANES = 128
SUB = 8
F32 = jnp.float32
BF16 = jnp.bfloat16


def split_np(table):
    high = table.astype(ml_dtypes.bfloat16)
    low = (table - high.astype(np.float64)).astype(ml_dtypes.bfloat16)
    return high, low


def dft_matrix(size):
    grid = np.outer(np.arange(size), np.arange(size)) % size
    angle = -2.0 * np.pi * grid / size
    cos, sin = np.cos(angle), np.sin(angle)
    return split_np(np.block([[cos, sin], [-sin, cos]]))


def twiddles(rows, cols, period, scale):
    angle = -2.0 * np.pi * (np.outer(np.arange(rows), np.arange(cols)) % period) / period
    return np.stack([np.cos(angle), np.sin(angle)]).astype(np.float32) * np.float32(scale)


def split(value):
    high = value.astype(BF16)
    return high, (value - high.astype(F32)).astype(BF16)


def times(value, re, im):
    return (value[0] * re - value[1] * im, value[0] * im + value[1] * re)


def add(a, b):
    return (a[0] + b[0], a[1] + b[1])


def sub(a, b):
    return (a[0] - b[0], a[1] - b[1])


def minus_i(a):
    return (a[1], -a[0])


def dft4(x):
    s0, d0, s1, d1 = add(x[0], x[2]), sub(x[0], x[2]), add(x[1], x[3]), minus_i(sub(x[1], x[3]))
    return [add(s0, s1), add(d0, d1), sub(s0, s1), sub(d0, d1)]


def dft8(x):
    half = math.sqrt(0.5)
    even, odd = dft4(x[0::2]), dft4(x[1::2])
    o1, o3 = odd[1], odd[3]
    odd = [
        odd[0],
        ((o1[0] + o1[1]) * half, (o1[1] - o1[0]) * half),
        minus_i(odd[2]),
        ((o3[1] - o3[0]) * half, (o3[0] + o3[1]) * -half),
    ]
    return [add(e, o) for e, o in zip(even, odd)] + [sub(e, o) for e, o in zip(even, odd)]


def group_transpose(vecs, lane):
    size = LANES // 4
    vecs = list(vecs)
    for dist in (1, 2):
        keep = (lane // (size * dist)) % 2 == 0
        for i in range(4):
            if i & dist:
                continue
            a, b = vecs[i], vecs[i + dist]
            vecs[i] = jnp.where(keep, a, pltpu.roll(b, size * dist, 1))
            vecs[i + dist] = jnp.where(keep, pltpu.roll(a, LANES - size * dist, 1), b)
    return vecs


def coarse_fft(half, rows, x_scr, taps_ref, tw_ref, wh_ref, wl_ref, u_scr, lh_scr, ll_scr, y_scr):
    tap_count = taps_ref.shape[0]
    cols = x_scr.shape[1]
    fold = cols // 4
    for r in range(fold):
        parts = []
        for q in range(4):
            a = r + fold * q
            acc = [None, None]
            for k in range(tap_count):
                tap = taps_ref[k : k + 1, a * LANES : (a + 1) * LANES]
                for comp in range(2):
                    term = tap * x_scr[comp, a, pl.ds(half * rows + k, rows, 1), :]
                    acc[comp] = term if k == 0 else acc[comp] + term
            parts.append(tuple(acc))
        for k1, value in enumerate(dft4(parts)):
            if r and k1:
                angle = -2.0 * math.pi * r * k1 / cols
                value = times(value, math.cos(angle), math.sin(angle))
            for comp in range(2):
                u_scr[comp, r, k1] = value[comp]
    for k1 in range(4):
        outs = dft8([(u_scr[0, r, k1], u_scr[1, r, k1]) for r in range(fold)])
        for k2, value in enumerate(outs):
            k = k1 + 4 * k2
            value = times(value, tw_ref[0, k : k + 1, :], tw_ref[1, k : k + 1, :])
            for comp in range(2):
                high, low = split(value[comp])
                lh_scr[pl.ds(k * rows, rows), comp * LANES : (comp + 1) * LANES] = high
                ll_scr[pl.ds(k * rows, rows), comp * LANES : (comp + 1) * LANES] = low
    step = 8 * rows
    for base in range(0, cols * rows, step):
        high, low = lh_scr[base : base + step], ll_scr[base : base + step]
        dot = partial(jnp.dot, preferred_element_type=F32)
        out = dot(high, wh_ref[...]) + (dot(low, wh_ref[...]) + dot(high, wl_ref[...]))
        for comp in range(2):
            piece = out[:, comp * LANES : (comp + 1) * LANES]
            y_scr[comp, base // rows : (base + step) // rows] = piece.reshape(8, rows, LANES)


def order_channels(half, order_ref, y_scr, put):
    cols = y_scr.shape[1]
    lane = lax.broadcasted_iota(jnp.int32, (SUB, LANES), 1)

    def step(q, carry):
        chan = jnp.broadcast_to(order_ref[pl.ds(q, 1), :], (SUB, LANES))
        source, which = chan // cols, chan % cols
        accs = [jnp.zeros((SUB, LANES), F32)] * 4
        for k in range(cols):
            mine = which == k
            for u in range(4):
                vec = y_scr[u // 2, k, (u % 2) * SUB : (u % 2 + 1) * SUB, :]
                got = jnp.take_along_axis(vec, source, axis=1, mode="promise_in_bounds")
                accs[u] = jnp.where(mine, got, accs[u])
        for r, vec in enumerate(group_transpose(accs, lane)):
            put(q, r, vec)
        return carry

    lax.fori_loop(0, order_ref.shape[0], step, 0)


def coarse_kernel(sig_ref, halo_ref, taps_ref, order_ref, tw_ref, wh_ref, wl_ref, out_ref,
                  x_scr, u_scr, lh_scr, ll_scr, y_scr, sem):
    slab = sig_ref.shape[2]
    cols = x_scr.shape[1]
    rows = slab // 2
    lead = halo_ref.shape[2]
    copies = []
    for comp in range(2):
        for a in range(cols):
            lanes = pl.ds(a * LANES, LANES)
            copies.append(pltpu.make_async_copy(
                sig_ref.at[comp, 0, :, lanes], x_scr.at[comp, a, pl.ds(0, slab), :], sem.at[0]))
            copies.append(pltpu.make_async_copy(
                halo_ref.at[comp, 0, :, lanes], x_scr.at[comp, a, pl.ds(slab, lead), :], sem.at[0]))
    for copy in copies:
        copy.start()
    for copy in copies:
        copy.wait()
    for half in range(2):
        coarse_fft(half, rows, x_scr, taps_ref, tw_ref, wh_ref, wl_ref, u_scr, lh_scr, ll_scr, y_scr)

        def put(q, r, vec, half=half):
            out_ref[4 * q + r, half] = vec

        order_channels(half, order_ref, y_scr, put)


def fine_fir(arr_ref, taps_ref, xs_scr, frames, per):
    lane = lax.broadcasted_iota(jnp.int32, (SUB, LANES), 1)
    row = lax.broadcasted_iota(jnp.int32, (SUB, LANES), 0)
    slots = LANES // 4
    spread = (lane % 4) * slots + lane // 4
    group = lane // slots
    slab = 4 * SUB

    def step(jb, carry):
        for k4 in range(4):
            jd = jb * 4 + k4
            for half in range(2):
                pick = k4 * slab + half * 2 * SUB + (group % 2) * SUB + row
                taps = [
                    jnp.take_along_axis(
                        jnp.broadcast_to(taps_ref[jb, k : k + 1, :], (SUB, LANES)), pick, axis=1,
                        mode="promise_in_bounds")
                    for k in range(min(frames, taps_ref.shape[1]))
                ]
                data = [arr_ref[g * per + jd, half] for g in range(frames)]
                outs = []
                for f in range(frames):
                    acc = None
                    for k in range(min(frames - f, len(taps))):
                        term = taps[k] * data[f + k]
                        acc = term if acc is None else acc + term
                    outs.append(acc)
                for u, vec in enumerate(group_transpose(outs, lane)):
                    vec = jnp.take_along_axis(vec, spread, axis=1, mode="promise_in_bounds")
                    base = pl.multiple_of(jd * slab + half * 2 * SUB + (u % 2) * SUB, SUB)
                    xs_scr[u // 2, pl.ds(base, SUB), :] = vec
        return carry

    lax.fori_loop(0, per // 4, step, 0)


def fine_fft(xs_scr, tw_ref, wh_ref, wl_ref, p_scr, out_ref):
    fold = xs_scr.shape[1] // LANES
    dot = partial(jnp.dot, preferred_element_type=F32)
    for a in range(fold):
        pieces = [jnp.transpose(xs_scr[comp, pl.ds(a, LANES, fold), :]) for comp in range(2)]
        high, low = split(jnp.concatenate(pieces, axis=1))
        out = dot(high, wh_ref[...]) + (dot(low, wh_ref[...]) + dot(high, wl_ref[...]))
        value = times((out[:, :LANES], out[:, LANES:]), tw_ref[0, a : a + 1, :], tw_ref[1, a : a + 1, :])
        for comp in range(2):
            p_scr[comp, a] = value[comp]
    frames = out_ref.shape[3]
    pack = SUB // frames

    def step(i, carry):
        rows = pl.ds(pl.multiple_of(i * SUB, SUB), SUB)
        outs = dft8([(p_scr[0, a, rows, :], p_scr[1, a, rows, :]) for a in range(fold)])
        for m1, value in enumerate(outs):
            for comp in range(2):
                out_ref[comp, 0, pl.ds(i * pack, pack), :, m1 * LANES : (m1 + 1) * LANES] = value[
                    comp].reshape(pack, frames, LANES)
        return carry

    lax.fori_loop(0, LANES // SUB, step, 0)


def fine_kernel(arr_ref, taps_ref, tw_ref, wh_ref, wl_ref, out_ref, xs_scr, p_scr):
    frames = out_ref.shape[3]
    fine_fir(arr_ref, taps_ref, xs_scr, frames, arr_ref.shape[0] // frames)
    fine_fft(xs_scr, tw_ref, wh_ref, wl_ref, p_scr, out_ref)


def shifted(value, axis, steps):
    count = lax.axis_size(axis)
    return lax.ppermute(value, axis, [(i, i + steps) for i in range(max(0, -steps), min(count, count - steps))])


def tables(width, fine):
    cols, fold = width // LANES, fine // LANES
    wh, wl = dft_matrix(LANES)
    tw_c = twiddles(cols, LANES, width, width ** -0.5)
    tw_f = twiddles(fold, LANES, fine, fine ** -0.5)
    return [jnp.asarray(t) for t in (wh, wl, tw_c, tw_f)]


def run_coarse(signal, halo, coarse_taps, order, wh, wl, tw_c, owners):
    slab, width = signal.shape[2:]
    cols = width // LANES
    rows = slab // 2
    vmem = pl.BlockSpec(memory_space=pltpu.VMEM)
    anym = pl.BlockSpec(memory_space=pl.ANY)
    return pl.pallas_call(
        coarse_kernel,
        out_shape=jax.ShapeDtypeStruct((owners, 2, SUB, LANES), F32),
        in_specs=[anym, anym, vmem, vmem, vmem, vmem, vmem],
        out_specs=vmem,
        scratch_shapes=[
            pltpu.VMEM((2, cols, slab + 16, LANES), F32),
            pltpu.VMEM((2, cols // 4, 4, rows, LANES), F32),
            pltpu.VMEM((cols * rows, 2 * LANES), BF16),
            pltpu.VMEM((cols * rows, 2 * LANES), BF16),
            pltpu.VMEM((2, cols, rows, LANES), F32),
            pltpu.SemaphoreType.DMA((1,)),
        ],
        name="coarse",
    )(signal, halo, coarse_taps, order, tw_c, wh, wl)


def run_fine(arrived, taps, wh, wl, tw_f, own, frames, fine):
    vmem = pl.BlockSpec(memory_space=pltpu.VMEM)
    return pl.pallas_call(
        fine_kernel,
        out_shape=jax.ShapeDtypeStruct((2, 1, own, frames, fine), F32),
        in_specs=[vmem] * 5,
        out_specs=vmem,
        scratch_shapes=[
            pltpu.VMEM((2, fine, LANES), F32),
            pltpu.VMEM((2, fine // LANES, LANES, LANES), F32),
        ],
        name="fine",
    )(arrived, taps, tw_f, wh, wl)


def body(signal, coarse_taps, fine_taps, channel_order):
    _, polars, slab, width = signal.shape
    tap_count, fine = fine_taps.shape
    owners = lax.axis_size(("tm", "sect"))
    own = width // owners
    frames = slab * owners // fine
    assert polars == 1 and slab == 4 * SUB and 4 * own == LANES and frames == 4 and tap_count == 16
    wh, wl, tw_c, tw_f = tables(width, fine)
    halo = shifted(signal[:, :, : tap_count - 1, :], ("tm", "sect"), -1)
    order = channel_order.reshape(width // LANES, LANES)
    blocks = run_coarse(signal, halo, coarse_taps, order, wh, wl, tw_c, owners)
    arrived = lax.all_to_all(blocks, ("tm", "sect"), split_axis=0, concat_axis=0, tiled=True)
    taps = jnp.swapaxes(fine_taps.reshape(tap_count, fine // LANES, LANES), 0, 1)
    return run_fine(arrived, taps, wh, wl, tw_f, own, frames, fine)


def solution(mesh):
    in_specs = (P(None, "pol", ("beam", "tm", "sect"), None), P(), P(), P())
    out_specs = P(None, "pol", ("beam", "tm", "sect"), None, None)
    return jax.shard_map(body, mesh=mesh, in_specs=in_specs, out_specs=out_specs, check_vma=False)
```

profile of v0, /device:TPU:94, one launch (start us, length us, event | category | flops | bytes accessed | tf_op | source)
XLA Modules:
  0.0 159.0 jit_solution(10121488595184280922)
XLA Ops:
  0.0 0.0 copy-start
  0.0 1.1 slice.3
  1.1 3.2 %collective-permute-start = (f32[2,1,15,4096]{3,2,1,0:T(8,128)S(1)}, f32[2,1,15,4096]{3,2,1,0:T(8,128)S(1)}, u32[]{:S(2)}, u32[]{:S(2)}) collective-permute-start(f32[2,1,15,4096]{3,2,1,0:T(8,128)S(1)} %slice.3), channel_id=1, source_target_pairs={{2,0},{4,2},{6,4},{8,6},{10,8},{12,10},{14,12},{16,14},{18,16},{20... | collective-permute-start | bytes 1474568 | tf_op jit(solution)/shard_map/ppermute | solution.py:247
  4.4 14.5 %collective-permute-done.halo_ref = f32[2,1,15,4096]{3,2,1,0:T(8,128)S(1)} collective-permute-done((f32[2,1,15,4096]{3,2,1,0:T(8,128)S(1)}, f32[2,1,15,4096]{3,2,1,0:T(8,128)S(1)}, u32[]{:S(2)}, u32[]{:S(2)}) %collective-permute-start) | collective-permute-done | bytes 491552 | tf_op jit(solution)/shard_map/ppermute | solution.py:247
  18.9 0.0 copy-start.2
  18.9 0.8 copy-done.2
  19.7 28.3 %coarse.1 = f32[128,2,8,128]{3,2,1,0:T(8,128)} custom-call(f32[2,1,32,4096]{3,2,1,0:T(8,128)} %sig_ref.1, f32[2,1,15,4096]{3,2,1,0:T(8,128)} %copy-done.2, f32[16,4096]{1,0:T(8,128)} %taps_ref.1, s32[32,128]{1,0:T(8,128)} %bitcast.8, f32[2,32,128]{2,1,0:T(8,128)} %constant.10.clone.tw_ref, bf16[256,256]{1,0:T(8,128)(2,1)} %constant.8.clone.wh_ref, ...), custom_call_target="tpu_custom_call" | custom-call | tf_op jit(solution)/shard_map/coarse/pallas_call | solution.py:264
  48.0 49.3 %all-to-all-start = ((f32[128,2,8,128]{3,2,1,0:T(8,128)}), f32[128,2,8,128]{3,2,1,0:T(8,128)S(1)}, u32[]{:S(2)}, u32[]{:S(2)}) async-start(f32[128,2,8,128]{3,2,1,0:T(8,128)} %coarse.1), calls=%async_computation | async-start | bytes 2097152 | tf_op jit(solution)/shard_map/all_to_all | solution.py:307
  97.3 0.0 copy-done
  97.3 0.6 bitcast_bitcast_fusion.taps_ref
  98.0 53.6 %all-to-all-done.arr_ref = f32[128,2,8,128]{3,2,1,0:T(8,128)S(1)} async-done(((f32[128,2,8,128]{3,2,1,0:T(8,128)}), f32[128,2,8,128]{3,2,1,0:T(8,128)S(1)}, u32[]{:S(2)}, u32[]{:S(2)}) %all-to-all-start) | async-done | bytes 1048608 | tf_op jit(solution)/shard_map/all_to_all | solution.py:307
  151.6 0.0 copy-start.1
  151.6 1.0 copy-done.1
  152.6 6.4 %fine.1 = f32[2,1,32,4,1024]{4,3,2,1,0:T(4,128)} custom-call(f32[128,2,8,128]{3,2,1,0:T(8,128)} %copy-done.1, f32[8,16,128]{2,1,0:T(8,128)} %bitcast_bitcast_fusion.taps_ref, f32[2,8,128]{2,1,0:T(8,128)} %constant.11.clone.tw_ref, bf16[256,256]{1,0:T(8,128)(2,1)} %constant.8.clone.wh_ref, bf16[256,256]{1,0:T(8,128)(2,1)} %constant.9.clone.wl_ref), custom_call_target="tpu_custom_call" | custom-call | tf_op jit(solution)/shard_map/fine/pallas_call | solution.py:283
Async XLA Ops:
  0.0 97.3 %copy-start = (f32[16,1024]{1,0:T(8,128)S(1)}, f32[16,1024]{1,0:T(8,128)}, u32[]{:S(2)}) copy-start(f32[16,1024]{1,0:T(8,128)} %param.10) | copy-start | bytes 196612
  1.1 17.8 %collective-permute-start = (f32[2,1,15,4096]{3,2,1,0:T(8,128)S(1)}, f32[2,1,15,4096]{3,2,1,0:T(8,128)S(1)}, u32[]{:S(2)}, u32[]{:S(2)}) collective-permute-start(f32[2,1,15,4096]{3,2,1,0:T(8,128)S(1)} %slice.3), channel_id=1, source_target_pairs={{2,0},{4,2},{6,4},{8,6},{10,8},{12,10},{14,12},{16,14},{18,16},{20... | collective-permute-start | bytes 1474568 | tf_op jit(solution)/shard_map/ppermute | solution.py:247
  18.9 0.8 copy-start.2
  48.0 103.6 %all-to-all-start = ((f32[128,2,8,128]{3,2,1,0:T(8,128)}), f32[128,2,8,128]{3,2,1,0:T(8,128)S(1)}, u32[]{:S(2)}, u32[]{:S(2)}) async-start(f32[128,2,8,128]{3,2,1,0:T(8,128)} %coarse.1), calls=%async_computation | async-start | bytes 2097152 | tf_op jit(solution)/shard_map/all_to_all | solution.py:307
  151.6 1.0 copy-start.1
where the time goes:
time: 159 us
  waiting for transfers between devices  68.2 us (43%)
  starting transfers between devices  52.6 us (33%)
  Pallas kernels  34.7 us (22%)
  local copies, waits for them, and re-layouts  3.5 us (2%)
    all_to_all x1, waiting for transfers between devices, body(): lax.all_to_all(blocks, ('tm', 'sect'), split_axis=0, concat_axis=0, tiled...  53.6 us
    all_to_all x1, starting transfers between devices, body(): lax.all_to_all(blocks, ('tm', 'sect'), split_axis=0, concat_axis=0, tiled...  49.3 us
    pallas_call x1, Pallas kernels, run_coarse(): pl.pallas_call(coarse_kernel, out_shape=jax.ShapeDtypeStruct((owners, 2,...  28.3 us
    ppermute x1, waiting for transfers between devices, shifted(): lax.ppermute(value, axis, [(i, i + steps) for i in range(max(0, -steps),...  14.5 us
    pallas_call x1, Pallas kernels, run_fine(): pl.pallas_call(fine_kernel, out_shape=jax.ShapeDtypeStruct((2, 1, own, fr...  6.39 us
    ppermute x1, starting transfers between devices, shifted(): lax.ppermute(value, axis, [(i, i + steps) for i in range(max(0, -steps),...  3.24 us
  transfers between devices with their start and end apart: 2, of which 2 were waited for; matrix products, arithmetic and copies ran while one was open for 0% of the time, Pallas kernels for 0%

commit v1 on v0

--- a/solution.py
+++ b/solution.py
@@ -170,7 +170,9 @@
         coarse_fft(half, rows, x_scr, taps_ref, tw_ref, wh_ref, wl_ref, u_scr, lh_scr, ll_scr, y_scr)
 
         def put(q, r, vec, half=half):
-            out_ref[4 * q + r, half] = vec
+            sects = out_ref.shape[1]
+            owner = 4 * q + r
+            out_ref[owner // sects, owner % sects, half] = vec
 
         order_channels(half, order_ref, y_scr, put)
 
@@ -242,6 +244,108 @@
     fine_fft(xs_scr, tw_ref, wh_ref, wl_ref, p_scr, out_ref)
 
 
+LAG = 3
+
+
+def exchange_kernel(blk_ref, arr_ref, relay, in_sem, below, far_send, far_recv, row_send, row_recv):
+    tms, sects = blk_ref.shape[:2]
+    x, z = lax.axis_index("sect"), lax.axis_index("tm")
+    last = tms - 1
+    barrier = pltpu.get_barrier_semaphore()
+    mesh_id = pl.DeviceIdType.MESH
+
+    def tell(sem, **where):
+        pl.semaphore_signal(sem, inc=1, device_id=where, device_id_type=mesh_id)
+
+    def loop(low, high, step):
+        lax.fori_loop(low, high, lambda i, carry: (step(i), carry)[1], 0)
+
+    def spread(source, j):
+        def send(i):
+            near = i // 2 + 1
+            to = lax.rem(x + near + (i % 2) * (sects - 2 * near), sects)
+            pltpu.make_async_remote_copy(
+                source.at[to], arr_ref.at[j, x], row_send.at[j], row_recv.at[j],
+                device_id={"sect": to}, device_id_type=mesh_id).start()
+
+        loop(0, sects - 1, send)
+        arr_ref[j, x] = source[x]
+
+    def across(j):
+        pltpu.make_async_remote_copy(
+            blk_ref.at[j], relay.at[z], far_send.at[j], far_recv.at[z],
+            device_id={"tm": j}, device_id_type=mesh_id).start()
+
+    loop(1, sects, lambda i: tell(barrier, sect=lax.rem(x + i, sects)))
+
+    @pl.when(z > 0)
+    def _():
+        tell(barrier, tm=z - 1)
+
+    pl.semaphore_wait(barrier, sects - 1 + (last - z + last - 1) // last)
+
+    @pl.when(z > 0)
+    def _():
+        pl.semaphore_wait(below, 1)
+
+    @pl.when(z < last)
+    def _():
+        tell(below, tm=z + 1)
+        loop(0, z, lambda j: tell(in_sem.at[z + 1], tm=j))
+
+    loop(0, z, across)
+    spread(blk_ref.at[z], z)
+
+    def step(s):
+        @pl.when(s < last - z)
+        def _():
+            @pl.when(s > 0)
+            def _():
+                pl.semaphore_wait(in_sem.at[z + 1 + s], 1)
+
+            across(z + 1 + s)
+
+        @pl.when(s >= LAG)
+        def _():
+            i = s - LAG
+            j = i + (i + tms - z) // tms
+            pltpu.make_async_copy(relay.at[j], relay.at[j], far_recv.at[j]).wait()
+            spread(relay.at[j], j)
+
+    loop(0, last + LAG, step)
+
+    def finish(j):
+        part = arr_ref.at[j, pl.ds(0, sects - 1)]
+        pltpu.make_async_copy(part, part, row_send.at[j]).wait()
+        pltpu.make_async_copy(part, part, row_recv.at[j]).wait()
+
+        @pl.when(j != z)
+        def _():
+            pltpu.make_async_copy(blk_ref.at[j], blk_ref.at[j], far_send.at[j]).wait()
+
+    loop(0, tms, finish)
+
+
+def run_exchange(blocks):
+    tms = blocks.shape[0]
+    vmem = pl.BlockSpec(memory_space=pltpu.VMEM)
+    dma = pltpu.SemaphoreType.DMA((tms,))
+    return pl.pallas_call(
+        exchange_kernel,
+        out_shape=jax.ShapeDtypeStruct(blocks.shape, F32),
+        in_specs=[vmem],
+        out_specs=vmem,
+        scratch_shapes=[
+            pltpu.VMEM(blocks.shape, F32),
+            pltpu.SemaphoreType.REGULAR((tms,)),
+            pltpu.SemaphoreType.REGULAR,
+            dma, dma, dma, dma,
+        ],
+        compiler_params=pltpu.CompilerParams(collective_id=0, has_side_effects=True),
+        name="exchange",
+    )(blocks)
+
+
 def shifted(value, axis, steps):
     count = lax.axis_size(axis)
     return lax.ppermute(value, axis, [(i, i + steps) for i in range(max(0, -steps), min(count, count - steps))])
@@ -255,7 +359,7 @@
     return [jnp.asarray(t) for t in (wh, wl, tw_c, tw_f)]
 
 
-def run_coarse(signal, halo, coarse_taps, order, wh, wl, tw_c, owners):
+def run_coarse(signal, halo, coarse_taps, order, wh, wl, tw_c, sects, tms):
     slab, width = signal.shape[2:]
     cols = width // LANES
     rows = slab // 2
@@ -263,7 +367,7 @@
     anym = pl.BlockSpec(memory_space=pl.ANY)
     return pl.pallas_call(
         coarse_kernel,
-        out_shape=jax.ShapeDtypeStruct((owners, 2, SUB, LANES), F32),
+        out_shape=jax.ShapeDtypeStruct((tms, sects, 2, SUB, LANES), F32),
         in_specs=[anym, anym, vmem, vmem, vmem, vmem, vmem],
         out_specs=vmem,
         scratch_shapes=[
@@ -303,8 +407,9 @@
     wh, wl, tw_c, tw_f = tables(width, fine)
     halo = shifted(signal[:, :, : tap_count - 1, :], ("tm", "sect"), -1)
     order = channel_order.reshape(width // LANES, LANES)
-    blocks = run_coarse(signal, halo, coarse_taps, order, wh, wl, tw_c, owners)
-    arrived = lax.all_to_all(blocks, ("tm", "sect"), split_axis=0, concat_axis=0, tiled=True)
+    sects, tms = lax.axis_size("sect"), lax.axis_size("tm")
+    blocks = run_coarse(signal, halo, coarse_taps, order, wh, wl, tw_c, sects, tms)
+    arrived = run_exchange(blocks).reshape(owners, 2, SUB, LANES)
     taps = jnp.swapaxes(fine_taps.reshape(tap_count, fine // LANES, LANES), 0, 1)
     return run_fine(arrived, taps, wh, wl, tw_f, own, frames, fine)
 

time: 159 us -> 139 us (0.87)
  the two profiles are of different devices: /device:TPU:94 before, /device:TPU:66 now
where the time goes in v1:
time: 139 us; the launch traced here: 138 us
  Pallas kernels  87.5 us (63%)
  starting transfers between devices  42.3 us (30%)
  waiting for transfers between devices  6.04 us (4%)
  local copies, waits for them, and re-layouts  2.53 us (2%)
    pallas_call x1, Pallas kernels, run_exchange(): pl.pallas_call(exchange_kernel, out_shape=jax.ShapeDtypeStruct(blocks.sha...  52.9 us
    ppermute x1, starting transfers between devices, shifted(): lax.ppermute(value, axis, [(i, i + steps) for i in range(max(0, -steps),...  42.3 us
    pallas_call x1, Pallas kernels, run_coarse(): pl.pallas_call(coarse_kernel, out_shape=jax.ShapeDtypeStruct((tms, sects,...  28.2 us
    pallas_call x1, Pallas kernels, run_fine(): pl.pallas_call(fine_kernel, out_shape=jax.ShapeDtypeStruct((2, 1, own, fr...  6.39 us
    ppermute x1, waiting for transfers between devices, shifted(): lax.ppermute(value, axis, [(i, i + steps) for i in range(max(0, -steps),...  6.04 us
  transfers between devices with their start and end apart: 1, of which 1 were waited for; matrix products, arithmetic and copies ran while one was open for 0% of the time, Pallas kernels for 0%

profile of v1, /device:TPU:66, one launch (start us, length us, event | category | flops | bytes accessed | tf_op | source)
XLA Modules:
  0.0 138.5 jit_solution(3320097210736378716)
XLA Ops:
  0.0 0.0 copy-start
  0.0 1.1 slice.3
  1.1 42.3 %collective-permute-start = (f32[2,1,15,4096]{3,2,1,0:T(8,128)S(1)}, f32[2,1,15,4096]{3,2,1,0:T(8,128)S(1)}, u32[]{:S(2)}, u32[]{:S(2)}) collective-permute-start(f32[2,1,15,4096]{3,2,1,0:T(8,128)S(1)} %slice.3), channel_id=1, source_target_pairs={{2,0},{4,2},{6,4},{8,6},{10,8},{12,10},{14,12},{16,14},{18,16},{20... | collective-permute-start | bytes 1474568 | tf_op jit(solution)/shard_map/ppermute | solution.py:351
  43.5 0.0 copy-done
  43.5 0.6 bitcast_bitcast_fusion.taps_ref
  44.1 6.0 %collective-permute-done.halo_ref = f32[2,1,15,4096]{3,2,1,0:T(8,128)S(1)} collective-permute-done((f32[2,1,15,4096]{3,2,1,0:T(8,128)S(1)}, f32[2,1,15,4096]{3,2,1,0:T(8,128)S(1)}, u32[]{:S(2)}, u32[]{:S(2)}) %collective-permute-start) | collective-permute-done | bytes 491552 | tf_op jit(solution)/shard_map/ppermute | solution.py:351
  50.1 0.0 copy-start.1
  50.1 0.8 copy-done.1
  50.9 28.2 %coarse.1.blk_ref = f32[16,8,2,8,128]{4,3,2,1,0:T(8,128)} custom-call(f32[2,1,32,4096]{3,2,1,0:T(8,128)} %sig_ref.1, f32[2,1,15,4096]{3,2,1,0:T(8,128)} %copy-done.1, f32[16,4096]{1,0:T(8,128)} %taps_ref.1, s32[32,128]{1,0:T(8,128)} %bitcast.10, f32[2,32,128]{2,1,0:T(8,128)} %constant.10.clone.tw_ref, bf16[256,256]{1,0:T(8,128)(2,1)} %constant.8.clone.wh_ref, ...), custom_call_target="tpu_custom_call" | custom-call | tf_op jit(solution)/shard_map/coarse/pallas_call | solution.py:368
  79.2 52.9 %exchange.1 = f32[16,8,2,8,128]{4,3,2,1,0:T(8,128)} custom-call(f32[16,8,2,8,128]{4,3,2,1,0:T(8,128)} %coarse.1.blk_ref), custom_call_target="tpu_custom_call" | custom-call | tf_op jit(solution)/shard_map/exchange/pallas_call | solution.py:333
  132.1 6.4 %fine.1 = f32[2,1,32,4,1024]{4,3,2,1,0:T(4,128)} custom-call(f32[128,2,8,128]{3,2,1,0:T(8,128)} %bitcast.9, f32[8,16,128]{2,1,0:T(8,128)} %bitcast_bitcast_fusion.taps_ref, f32[2,8,128]{2,1,0:T(8,128)} %constant.11.clone.tw_ref, bf16[256,256]{1,0:T(8,128)(2,1)} %constant.8.clone.wh_ref, bf16[256,256]{1,0:T(8,128)(2,1)} %constant.9.clone.wl_ref), custom_call_target="tpu_custom_call" | custom-call | tf_op jit(solution)/shard_map/fine/pallas_call | solution.py:387
Async XLA Ops:
  0.0 43.5 %copy-start = (f32[16,1024]{1,0:T(8,128)S(1)}, f32[16,1024]{1,0:T(8,128)}, u32[]{:S(2)}) copy-start(f32[16,1024]{1,0:T(8,128)} %param.10) | copy-start | bytes 196612
  1.1 49.0 %collective-permute-start = (f32[2,1,15,4096]{3,2,1,0:T(8,128)S(1)}, f32[2,1,15,4096]{3,2,1,0:T(8,128)S(1)}, u32[]{:S(2)}, u32[]{:S(2)}) collective-permute-start(f32[2,1,15,4096]{3,2,1,0:T(8,128)S(1)} %slice.3), channel_id=1, source_target_pairs={{2,0},{4,2},{6,4},{8,6},{10,8},{12,10},{14,12},{16,14},{18,16},{20... | collective-permute-start | bytes 1474568 | tf_op jit(solution)/shard_map/ppermute | solution.py:351
  50.1 0.8 copy-start.1

commit v2 on v0

--- a/solution.py
+++ b/solution.py
@@ -127,52 +127,35 @@
             y_scr[comp, base // rows : (base + step) // rows] = piece.reshape(8, rows, LANES)
 
 
-def order_channels(half, order_ref, y_scr, put):
-    cols = y_scr.shape[1]
+def order_channels(index_ref, y_scr, z_scr, g_scr, put):
+    cols, rows = y_scr.shape[1:3]
     lane = lax.broadcasted_iota(jnp.int32, (SUB, LANES), 1)
-
-    def step(q, carry):
-        chan = jnp.broadcast_to(order_ref[pl.ds(q, 1), :], (SUB, LANES))
-        source, which = chan // cols, chan % cols
-        accs = [jnp.zeros((SUB, LANES), F32)] * 4
-        for k in range(cols):
-            mine = which == k
-            for u in range(4):
-                vec = y_scr[u // 2, k, (u % 2) * SUB : (u % 2 + 1) * SUB, :]
-                got = jnp.take_along_axis(vec, source, axis=1, mode="promise_in_bounds")
-                accs[u] = jnp.where(mine, got, accs[u])
-        for r, vec in enumerate(group_transpose(accs, lane)):
-            put(q, r, vec)
+    for k in range(cols):
+        both = jnp.concatenate([y_scr[0, k], y_scr[1, k]], axis=0)
+        z_scr[k * LANES : (k + 1) * LANES, :] = jnp.transpose(jnp.concatenate([both] * 4, axis=0))
+    row_lane = lax.broadcasted_iota(jnp.int32, (1, LANES), 1)
+    group = LANES // 4
+    chunk = 16
+
+    def step(part, carry):
+        def fetch(i, inner):
+            for u in range(chunk):
+                at = i * chunk + u
+                got = [z_scr[pl.ds(index_ref[(part * 4 + h) * LANES + at], 1), :] for h in range(4)]
+                low = jnp.where(row_lane < group, got[0], got[1])
+                high = jnp.where(row_lane < 3 * group, got[2], got[3])
+                g_scr[pl.ds(at, 1), :] = jnp.where(row_lane < 2 * group, low, high)
+            return inner
+
+        lax.fori_loop(0, LANES // chunk, fetch, 0)
+        turned = jnp.transpose(g_scr[...])
+        for h in range(4):
+            vecs = [turned[(h * 4 + u) * SUB : (h * 4 + u + 1) * SUB] for u in range(4)]
+            for r, vec in enumerate(group_transpose(vecs, lane)):
+                put(part * 4 + h, r, vec)
         return carry
 
-    lax.fori_loop(0, order_ref.shape[0], step, 0)
-
-
-def coarse_kernel(sig_ref, halo_ref, taps_ref, order_ref, tw_ref, wh_ref, wl_ref, out_ref,
-                  x_scr, u_scr, lh_scr, ll_scr, y_scr, sem):
-    slab = sig_ref.shape[2]
-    cols = x_scr.shape[1]
-    rows = slab // 2
-    lead = halo_ref.shape[2]
-    copies = []
-    for comp in range(2):
-        for a in range(cols):
-            lanes = pl.ds(a * LANES, LANES)
-            copies.append(pltpu.make_async_copy(
-                sig_ref.at[comp, 0, :, lanes], x_scr.at[comp, a, pl.ds(0, slab), :], sem.at[0]))
-            copies.append(pltpu.make_async_copy(
-                halo_ref.at[comp, 0, :, lanes], x_scr.at[comp, a, pl.ds(slab, lead), :], sem.at[0]))
-    for copy in copies:
-        copy.start()
-    for copy in copies:
-        copy.wait()
-    for half in range(2):
-        coarse_fft(half, rows, x_scr, taps_ref, tw_ref, wh_ref, wl_ref, u_scr, lh_scr, ll_scr, y_scr)
-
-        def put(q, r, vec, half=half):
-            out_ref[4 * q + r, half] = vec
-
-        order_channels(half, order_ref, y_scr, put)
+    lax.fori_loop(0, cols // 4, step, 0)
 
 
 def fine_fir(arr_ref, taps_ref, xs_scr, frames, per):
@@ -194,7 +177,7 @@
                         mode="promise_in_bounds")
                     for k in range(min(frames, taps_ref.shape[1]))
                 ]
-                data = [arr_ref[g * per + jd, half] for g in range(frames)]
+                data = [arr_ref[half, g * per + jd] for g in range(frames)]
                 outs = []
                 for f in range(frames):
                     acc = None
@@ -238,13 +221,198 @@
 
 def fine_kernel(arr_ref, taps_ref, tw_ref, wh_ref, wl_ref, out_ref, xs_scr, p_scr):
     frames = out_ref.shape[3]
-    fine_fir(arr_ref, taps_ref, xs_scr, frames, arr_ref.shape[0] // frames)
+    fine_fir(arr_ref, taps_ref, xs_scr, frames, arr_ref.shape[1] // frames)
     fine_fft(xs_scr, tw_ref, wh_ref, wl_ref, p_scr, out_ref)
 
 
-def shifted(value, axis, steps):
-    count = lax.axis_size(axis)
-    return lax.ppermute(value, axis, [(i, i + steps) for i in range(max(0, -steps), min(count, count - steps))])
+LAG = 3
+
+
+def front_kernel(sig_ref, taps_ref, index_ref, tw_ref, wh_ref, wl_ref, arr_ref,
+                 x_scr, halo, u_scr, lh_scr, ll_scr, y_scr, z_scr, g_scr, blk, relay,
+                 load_sem, halo_sem, in_sem, below, far_send, far_recv, row_send, row_recv):
+    slab = sig_ref.shape[2]
+    cols = x_scr.shape[1]
+    rows = slab // 2
+    lead = halo.shape[1]
+    tms, sects = blk.shape[1:3]
+    x, z = lax.axis_index("sect"), lax.axis_index("tm")
+    last, edge = tms - 1, sects - 1
+    barrier = pltpu.get_barrier_semaphore()
+    mesh_id = pl.DeviceIdType.MESH
+
+    def tell(sem, **where):
+        pl.semaphore_signal(sem, inc=1, device_id=where, device_id_type=mesh_id)
+
+    def loop(low, high, step):
+        lax.fori_loop(low, high, lambda i, carry: (step(i), carry)[1], 0)
+
+    def load(a):
+        lanes = pl.ds(pl.multiple_of(a * LANES, LANES), LANES)
+        for comp in range(2):
+            pltpu.make_async_copy(
+                sig_ref.at[comp, 0, :, lanes], x_scr.at[comp, a, pl.ds(0, slab), :], load_sem).start()
+
+    loop(0, cols, load)
+
+    loop(1, sects, lambda i: tell(barrier, sect=lax.rem(x + i, sects)))
+
+    @pl.when(z > 0)
+    def _():
+        tell(barrier, tm=z - 1)
+
+    @pl.when(jnp.logical_and(x == edge, z < last))
+    def _():
+        tell(barrier, tm=z + 1, sect=0)
+
+    not_last = (last - z + last - 1) // last
+    wraps = (1 - (x + edge) // sects) * ((z + last - 1) // last)
+    has_next = z * sects + x < tms * sects - 1
+
+    def halo_copy():
+        return pltpu.make_async_remote_copy(
+            sig_ref.at[:, 0, pl.ds(0, lead), :], halo, halo_sem.at[0], halo_sem.at[1],
+            device_id={"tm": z - (1 - (x + edge) // sects), "sect": lax.rem(x + edge, sects)},
+            device_id_type=mesh_id)
+
+    def spread(source, half, j):
+        def send(i):
+            near = i // 2 + 1
+            to = lax.rem(x + near + (i % 2) * (sects - 2 * near), sects)
+            pltpu.make_async_remote_copy(
+                source.at[to], arr_ref.at[half, j, x], row_send.at[half, j], row_recv.at[half, j],
+                device_id={"sect": to}, device_id_type=mesh_id).start()
+
+        loop(0, edge, send)
+        arr_ref[half, j, x] = source[x]
+
+    def across(half, j):
+        pltpu.make_async_remote_copy(
+            blk.at[half, j], relay.at[half, z], far_send.at[half, j], far_recv.at[half, z],
+            device_id={"tm": j}, device_id_type=mesh_id).start()
+
+    def half_step(half):
+        @pl.when(half == 0)
+        def _():
+            done = x_scr.at[:, :, pl.ds(0, slab), :]
+            pltpu.make_async_copy(done, done, load_sem).wait()
+
+        @pl.when(half == 1)
+        def _():
+            @pl.when(has_next)
+            def _():
+                pltpu.make_async_copy(halo, halo, halo_sem.at[1]).wait()
+                for comp in range(2):
+                    for a in range(cols):
+                        x_scr[comp, a, pl.ds(slab, lead), :] = halo[comp, :, a * LANES : (a + 1) * LANES]
+
+            @pl.when(jnp.logical_not(has_next))
+            def _():
+                x_scr[:, :, pl.ds(slab, lead), :] = jnp.zeros((2, cols, lead, LANES), F32)
+
+        coarse_fft(half, rows, x_scr, taps_ref, tw_ref, wh_ref, wl_ref, u_scr, lh_scr, ll_scr, y_scr)
+
+        def put(q, r, vec):
+            owner = 4 * q + r
+            blk[half, owner // sects, owner % sects] = vec
+
+        order_channels(index_ref, y_scr, z_scr, g_scr, put)
+
+        @pl.when(half == 0)
+        def _():
+            pl.semaphore_wait(barrier, edge + not_last + wraps)
+
+            @pl.when(z * sects + x > 0)
+            def _():
+                halo_copy().start()
+
+            @pl.when(z > 0)
+            def _():
+                pl.semaphore_wait(below, 1)
+
+            @pl.when(z < last)
+            def _():
+                tell(below, tm=z + 1)
+                loop(0, z, lambda j: tell(in_sem.at[z + 1], tm=j))
+
+        loop(0, z, lambda j: across(half, j))
+        spread(blk.at[half, z], half, z)
+
+    loop(0, 2, half_step)
+
+    def step(s):
+        @pl.when(s < last - z)
+        def _():
+            @pl.when(s > 0)
+            def _():
+                pl.semaphore_wait(in_sem.at[z + 1 + s], 1)
+
+            for half in range(2):
+                across(half, z + 1 + s)
+
+        @pl.when(s >= LAG)
+        def _():
+            i = s - LAG
+            j = i + (i + tms - z) // tms
+            for half in range(2):
+                landed = relay.at[half, j]
+                pltpu.make_async_copy(landed, landed, far_recv.at[half, j]).wait()
+                spread(landed, half, j)
+
+    loop(0, last + LAG, step)
+
+    def finish(j):
+        for half in range(2):
+            part = arr_ref.at[half, j, pl.ds(0, edge)]
+            pltpu.make_async_copy(part, part, row_send.at[half, j]).wait()
+            pltpu.make_async_copy(part, part, row_recv.at[half, j]).wait()
+
+            @pl.when(j != z)
+            def _():
+                sent = blk.at[half, j]
+                pltpu.make_async_copy(sent, sent, far_send.at[half, j]).wait()
+
+    loop(0, tms, finish)
+
+    @pl.when(z * sects + x > 0)
+    def _():
+        pltpu.make_async_copy(halo, halo, halo_sem.at[0]).wait()
+
+
+def run_front(signal, coarse_taps, index, wh, wl, tw_c, sects, tms):
+    slab, width = signal.shape[2:]
+    cols = width // LANES
+    rows = slab // 2
+    vmem = pl.BlockSpec(memory_space=pltpu.VMEM)
+    anym = pl.BlockSpec(memory_space=pl.ANY)
+    smem = pl.BlockSpec(memory_space=pltpu.SMEM)
+    dma = pltpu.SemaphoreType.DMA((2, tms))
+    blocks = (2, tms, sects, SUB, LANES)
+    return pl.pallas_call(
+        front_kernel,
+        out_shape=jax.ShapeDtypeStruct(blocks, F32),
+        in_specs=[anym, vmem, smem, vmem, vmem, vmem],
+        out_specs=vmem,
+        scratch_shapes=[
+            pltpu.VMEM((2, cols, slab + rows, LANES), F32),
+            pltpu.VMEM((2, rows, width), F32),
+            pltpu.VMEM((2, cols // 4, 4, rows, LANES), F32),
+            pltpu.VMEM((cols * rows, 2 * LANES), BF16),
+            pltpu.VMEM((cols * rows, 2 * LANES), BF16),
+            pltpu.VMEM((2, cols, rows, LANES), F32),
+            pltpu.VMEM((width, LANES), F32),
+            pltpu.VMEM((LANES, LANES), F32),
+            pltpu.VMEM(blocks, F32),
+            pltpu.VMEM(blocks, F32),
+            pltpu.SemaphoreType.DMA,
+            pltpu.SemaphoreType.DMA((2,)),
+            pltpu.SemaphoreType.REGULAR((tms,)),
+            pltpu.SemaphoreType.REGULAR,
+            dma, dma, dma, dma,
+        ],
+        compiler_params=pltpu.CompilerParams(collective_id=0, has_side_effects=True),
+        name="front",
+    )(signal, coarse_taps, index, tw_c, wh, wl)
 
 
 def tables(width, fine):
@@ -253,29 +421,6 @@
     tw_c = twiddles(cols, LANES, width, width ** -0.5)
     tw_f = twiddles(fold, LANES, fine, fine ** -0.5)
     return [jnp.asarray(t) for t in (wh, wl, tw_c, tw_f)]
-
-
-def run_coarse(signal, halo, coarse_taps, order, wh, wl, tw_c, owners):
-    slab, width = signal.shape[2:]
-    cols = width // LANES
-    rows = slab // 2
-    vmem = pl.BlockSpec(memory_space=pltpu.VMEM)
-    anym = pl.BlockSpec(memory_space=pl.ANY)
-    return pl.pallas_call(
-        coarse_kernel,
-        out_shape=jax.ShapeDtypeStruct((owners, 2, SUB, LANES), F32),
-        in_specs=[anym, anym, vmem, vmem, vmem, vmem, vmem],
-        out_specs=vmem,
-        scratch_shapes=[
-            pltpu.VMEM((2, cols, slab + 16, LANES), F32),
-            pltpu.VMEM((2, cols // 4, 4, rows, LANES), F32),
-            pltpu.VMEM((cols * rows, 2 * LANES), BF16),
-            pltpu.VMEM((cols * rows, 2 * LANES), BF16),
-            pltpu.VMEM((2, cols, rows, LANES), F32),
-            pltpu.SemaphoreType.DMA((1,)),
-        ],
-        name="coarse",
-    )(signal, halo, coarse_taps, order, tw_c, wh, wl)
 
 
 def run_fine(arrived, taps, wh, wl, tw_f, own, frames, fine):
@@ -301,10 +446,12 @@
     frames = slab * owners // fine
     assert polars == 1 and slab == 4 * SUB and 4 * own == LANES and frames == 4 and tap_count == 16
     wh, wl, tw_c, tw_f = tables(width, fine)
-    halo = shifted(signal[:, :, : tap_count - 1, :], ("tm", "sect"), -1)
-    order = channel_order.reshape(width // LANES, LANES)
-    blocks = run_coarse(signal, halo, coarse_taps, order, wh, wl, tw_c, owners)
-    arrived = lax.all_to_all(blocks, ("tm", "sect"), split_axis=0, concat_axis=0, tiled=True)
+    cols = width // LANES
+    index = channel_order % cols * LANES + channel_order // cols
+    sects, tms = lax.axis_size("sect"), lax.axis_size("tm")
+    assert tap_count - 1 <= slab // 2
+    blocks = run_front(signal, coarse_taps, index, wh, wl, tw_c, sects, tms)
+    arrived = blocks.reshape(2, owners, SUB, LANES)
     taps = jnp.swapaxes(fine_taps.reshape(tap_count, fine // LANES, LANES), 0, 1)
     return run_fine(arrived, taps, wh, wl, tw_f, own, frames, fine)
 

time: 159 us -> 119 us (0.75)
  the two profiles are of different devices: /device:TPU:94 before, /device:TPU:66 now
where the time goes in v2:
time: 119 us
  Pallas kernels  116 us (97%)
  other arithmetic  1.37 us (1%)
    pallas_call x1, Pallas kernels, run_front(): pl.pallas_call(front_kernel, out_shape=jax.ShapeDtypeStruct(blocks, F32),...  110 us
    pallas_call x1, Pallas kernels, run_fine(): pl.pallas_call(fine_kernel, out_shape=jax.ShapeDtypeStruct((2, 1, own, fr...  6.39 us

profile of v2, /device:TPU:66, one launch (start us, length us, event | category | flops | bytes accessed | tf_op | source)
XLA Modules:
  0.0 118.5 jit_solution(11942349114982133704)
XLA Ops:
  0.0 0.0 copy-start
  0.0 1.4 %fusion.1.index_ref = s32[4096]{0:T(1024)} fusion(s32[4096]{0:T(1024)} %param.11), kind=kLoop, calls=%fused_computation.7 | loop fusion | flops 86016 | bytes 32768 | tf_op jit(solution)/shard_map/add | solution.py:450
  1.4 0.0 copy-done
  1.4 0.6 bitcast_bitcast_fusion.taps_ref
  2.0 110.1 %front.1 = f32[2,16,8,8,128]{4,3,2,1,0:T(8,128)} custom-call(f32[2,1,32,4096]{3,2,1,0:T(8,128)} %sig_ref.1, f32[16,4096]{1,0:T(8,128)} %taps_ref.1, s32[4096]{0:T(1024)} %fusion.1.index_ref, f32[2,32,128]{2,1,0:T(8,128)} %constant.40.clone.tw_ref, bf16[256,256]{1,0:T(8,128)(2,1)} %constant.38.clone.wh_ref, bf16[256,256]{1,0:T(8,128)(2,1)} %constant.39.clone.wl_ref), custom_call_target="tpu_custom_call" | custom-call | tf_op jit(solution)/shard_map/front/pallas_call | solution.py:391
  112.1 6.4 %fine.1 = f32[2,1,32,4,1024]{4,3,2,1,0:T(4,128)} custom-call(f32[2,128,8,128]{3,2,1,0:T(8,128)} %bitcast.8, f32[8,16,128]{2,1,0:T(8,128)} %bitcast_bitcast_fusion.taps_ref, f32[2,8,128]{2,1,0:T(8,128)} %constant.41.clone.tw_ref, bf16[256,256]{1,0:T(8,128)(2,1)} %constant.38.clone.wh_ref, bf16[256,256]{1,0:T(8,128)(2,1)} %constant.39.clone.wl_ref), custom_call_target="tpu_custom_call" | custom-call | tf_op jit(solution)/shard_map/fine/pallas_call | solution.py:428
Async XLA Ops:
  0.0 1.4 %copy-start = (f32[16,1024]{1,0:T(8,128)S(1)}, f32[16,1024]{1,0:T(8,128)}, u32[]{:S(2)}) copy-start(f32[16,1024]{1,0:T(8,128)} %param.10) | copy-start | bytes 196612

commit v3 on v2

--- a/solution.py
+++ b/solution.py
@@ -139,12 +139,13 @@
 
     def step(part, carry):
         def fetch(i, inner):
+            lists = [index_ref.at[pl.ds((part * 4 + h) * LANES + i * chunk, chunk)] for h in range(4)]
+            spot = g_scr.at[pl.ds(pl.multiple_of(i * chunk, chunk), chunk), :]
             for u in range(chunk):
-                at = i * chunk + u
-                got = [z_scr[pl.ds(index_ref[(part * 4 + h) * LANES + at], 1), :] for h in range(4)]
+                got = [z_scr[pl.ds(lists[h][u], 1), :] for h in range(4)]
                 low = jnp.where(row_lane < group, got[0], got[1])
                 high = jnp.where(row_lane < 3 * group, got[2], got[3])
-                g_scr[pl.ds(at, 1), :] = jnp.where(row_lane < 2 * group, low, high)
+                spot[u : u + 1, :] = jnp.where(row_lane < 2 * group, low, high)
             return inner
 
         lax.fori_loop(0, LANES // chunk, fetch, 0)
@@ -162,7 +163,6 @@
     lane = lax.broadcasted_iota(jnp.int32, (SUB, LANES), 1)
     row = lax.broadcasted_iota(jnp.int32, (SUB, LANES), 0)
     slots = LANES // 4
-    spread = (lane % 4) * slots + lane // 4
     group = lane // slots
     slab = 4 * SUB
 
@@ -186,7 +186,6 @@
                         acc = term if acc is None else acc + term
                     outs.append(acc)
                 for u, vec in enumerate(group_transpose(outs, lane)):
-                    vec = jnp.take_along_axis(vec, spread, axis=1, mode="promise_in_bounds")
                     base = pl.multiple_of(jd * slab + half * 2 * SUB + (u % 2) * SUB, SUB)
                     xs_scr[u // 2, pl.ds(base, SUB), :] = vec
         return carry
@@ -196,6 +195,7 @@
 
 def fine_fft(xs_scr, tw_ref, wh_ref, wl_ref, p_scr, out_ref):
     fold = xs_scr.shape[1] // LANES
+    slots, frames = out_ref.shape[2:4]
     dot = partial(jnp.dot, preferred_element_type=F32)
     for a in range(fold):
         pieces = [jnp.transpose(xs_scr[comp, pl.ds(a, LANES, fold), :]) for comp in range(2)]
@@ -203,8 +203,8 @@
         out = dot(high, wh_ref[...]) + (dot(low, wh_ref[...]) + dot(high, wl_ref[...]))
         value = times((out[:, :LANES], out[:, LANES:]), tw_ref[0, a : a + 1, :], tw_ref[1, a : a + 1, :])
         for comp in range(2):
-            p_scr[comp, a] = value[comp]
-    frames = out_ref.shape[3]
+            for f in range(frames):
+                p_scr[comp, a, pl.ds(f, slots, frames), :] = value[comp][f * slots : (f + 1) * slots]
     pack = SUB // frames
 
     def step(i, carry):
@@ -225,12 +225,12 @@
     fine_fft(xs_scr, tw_ref, wh_ref, wl_ref, p_scr, out_ref)
 
 
-LAG = 3
+EARLY = 5
 
 
 def front_kernel(sig_ref, taps_ref, index_ref, tw_ref, wh_ref, wl_ref, arr_ref,
-                 x_scr, halo, u_scr, lh_scr, ll_scr, y_scr, z_scr, g_scr, blk, relay,
-                 load_sem, halo_sem, in_sem, below, far_send, far_recv, row_send, row_recv):
+                 x_scr, halo, first, second, u_scr, lh_scr, ll_scr, y_scr, z_scr, g_scr, blk, relay,
+                 load_sem, halo_sem, leg_sem, in_sem, below, far_send, far_recv, row_send, row_recv):
     slab = sig_ref.shape[2]
     cols = x_scr.shape[1]
     rows = slab // 2
@@ -261,19 +261,34 @@
     def _():
         tell(barrier, tm=z - 1)
 
-    @pl.when(jnp.logical_and(x == edge, z < last))
-    def _():
-        tell(barrier, tm=z + 1, sect=0)
-
     not_last = (last - z + last - 1) // last
-    wraps = (1 - (x + edge) // sects) * ((z + last - 1) // last)
-    has_next = z * sects + x < tms * sects - 1
+    width = halo.shape[2]
+    piece = width // sects
+    inner, middle = x > 0, x < edge
+    lower, upper = z > 0, z < last
+    both = jnp.logical_and
 
     def halo_copy():
         return pltpu.make_async_remote_copy(
             sig_ref.at[:, 0, pl.ds(0, lead), :], halo, halo_sem.at[0], halo_sem.at[1],
-            device_id={"tm": z - (1 - (x + edge) // sects), "sect": lax.rem(x + edge, sects)},
-            device_id_type=mesh_id)
+            device_id={"sect": x - 1}, device_id_type=mesh_id)
+
+    def to_row(i):
+        return pltpu.make_async_remote_copy(
+            sig_ref.at[:, 0, pl.ds(0, lead), pl.ds(pl.multiple_of(i * piece, piece), piece)], first,
+            leg_sem.at[0], leg_sem.at[1], device_id={"sect": i}, device_id_type=mesh_id)
+
+    def down(source):
+        return pltpu.make_async_remote_copy(
+            source, second, leg_sem.at[2], leg_sem.at[3], device_id={"tm": z - 1}, device_id_type=mesh_id)
+
+    def to_edge():
+        return pltpu.make_async_remote_copy(
+            second, halo.at[:, :, pl.ds(pl.multiple_of(x * piece, piece), piece)],
+            leg_sem.at[4], halo_sem.at[1], device_id={"sect": edge}, device_id_type=mesh_id)
+
+    def wait_for(part, sem):
+        pltpu.make_async_copy(part, part, sem).wait()
 
     def spread(source, half, j):
         def send(i):
@@ -296,17 +311,48 @@
         def _():
             done = x_scr.at[:, :, pl.ds(0, slab), :]
             pltpu.make_async_copy(done, done, load_sem).wait()
+            pl.semaphore_wait(barrier, edge + not_last)
+
+            @pl.when(both(x == 0, lower))
+            def _():
+                loop(1, sects, lambda i: to_row(sects - i).start())
+
+            @pl.when(inner)
+            def _():
+                halo_copy().start()
+
+            @pl.when(lower)
+            def _():
+                pl.semaphore_wait(below, 1)
+
+            @pl.when(z < last)
+            def _():
+                tell(below, tm=z + 1)
+                loop(0, z, lambda j: tell(in_sem.at[z + 1], tm=j))
+
+            @pl.when(both(x == 0, lower))
+            def _():
+                down(sig_ref.at[:, 0, pl.ds(0, lead), pl.ds(0, piece)]).start()
 
         @pl.when(half == 1)
         def _():
-            @pl.when(has_next)
-            def _():
-                pltpu.make_async_copy(halo, halo, halo_sem.at[1]).wait()
+            @pl.when(middle)
+            def _():
+                wait_for(halo, halo_sem.at[1])
+
+            @pl.when(both(x == edge, upper))
+            def _():
+                wait_for(second, leg_sem.at[3])
+                wait_for(halo.at[:, :, pl.ds(0, width - piece)], halo_sem.at[1])
+                halo[:, :, width - piece :] = second[...]
+
+            @pl.when(jnp.logical_or(middle, upper))
+            def _():
                 for comp in range(2):
                     for a in range(cols):
                         x_scr[comp, a, pl.ds(slab, lead), :] = halo[comp, :, a * LANES : (a + 1) * LANES]
 
-            @pl.when(jnp.logical_not(has_next))
+            @pl.when(both(x == edge, z == last))
             def _():
                 x_scr[:, :, pl.ds(slab, lead), :] = jnp.zeros((2, cols, lead, LANES), F32)
 
@@ -318,48 +364,46 @@
 
         order_channels(index_ref, y_scr, z_scr, g_scr, put)
 
-        @pl.when(half == 0)
+        @pl.when(both(half == 0, both(inner, lower)))
         def _():
-            pl.semaphore_wait(barrier, edge + not_last + wraps)
-
-            @pl.when(z * sects + x > 0)
-            def _():
-                halo_copy().start()
-
-            @pl.when(z > 0)
-            def _():
-                pl.semaphore_wait(below, 1)
-
-            @pl.when(z < last)
-            def _():
-                tell(below, tm=z + 1)
-                loop(0, z, lambda j: tell(in_sem.at[z + 1], tm=j))
+            wait_for(first, leg_sem.at[1])
+            down(first).start()
+
+        @pl.when(both(half == 1, both(middle, upper)))
+        def _():
+            wait_for(second, leg_sem.at[3])
+            to_edge().start()
 
         loop(0, z, lambda j: across(half, j))
         spread(blk.at[half, z], half, z)
 
+        def early(s):
+            @pl.when(jnp.logical_and(half == 0, s > 0))
+            def _():
+                pl.semaphore_wait(in_sem.at[z + 1 + s], 1)
+
+            across(half, z + 1 + s)
+
+        loop(0, jnp.minimum(EARLY, last - z), early)
+
+
     loop(0, 2, half_step)
 
-    def step(s):
-        @pl.when(s < last - z)
-        def _():
-            @pl.when(s > 0)
-            def _():
-                pl.semaphore_wait(in_sem.at[z + 1 + s], 1)
-
-            for half in range(2):
-                across(half, z + 1 + s)
-
-        @pl.when(s >= LAG)
-        def _():
-            i = s - LAG
-            j = i + (i + tms - z) // tms
-            for half in range(2):
-                landed = relay.at[half, j]
-                pltpu.make_async_copy(landed, landed, far_recv.at[half, j]).wait()
-                spread(landed, half, j)
-
-    loop(0, last + LAG, step)
+    def later(s):
+        pl.semaphore_wait(in_sem.at[z + 1 + s], 1)
+        for half in range(2):
+            across(half, z + 1 + s)
+
+    loop(EARLY, last - z, later)
+
+    def hand_on(i):
+        j = i + (i + tms - z) // tms
+        for half in range(2):
+            landed = relay.at[half, j]
+            pltpu.make_async_copy(landed, landed, far_recv.at[half, j]).wait()
+            spread(landed, half, j)
+
+    loop(0, last, hand_on)
 
     def finish(j):
         for half in range(2):
@@ -374,12 +418,24 @@
 
     loop(0, tms, finish)
 
-    @pl.when(z * sects + x > 0)
+    @pl.when(inner)
     def _():
-        pltpu.make_async_copy(halo, halo, halo_sem.at[0]).wait()
-
-
-def run_front(signal, coarse_taps, index, wh, wl, tw_c, sects, tms):
+        wait_for(halo, halo_sem.at[0])
+
+    @pl.when(both(x == 0, lower))
+    def _():
+        wait_for(halo.at[:, :, pl.ds(0, width - piece)], leg_sem.at[0])
+
+    @pl.when(lower)
+    def _():
+        wait_for(second, leg_sem.at[2])
+
+    @pl.when(both(middle, upper))
+    def _():
+        wait_for(second, leg_sem.at[4])
+
+
+def run_front(signal, coarse_taps, channel_order, wh, wl, tw_c, sects, tms):
     slab, width = signal.shape[2:]
     cols = width // LANES
     rows = slab // 2
@@ -396,6 +452,8 @@
         scratch_shapes=[
             pltpu.VMEM((2, cols, slab + rows, LANES), F32),
             pltpu.VMEM((2, rows, width), F32),
+            pltpu.VMEM((2, rows, width // sects), F32),
+            pltpu.VMEM((2, rows, width // sects), F32),
             pltpu.VMEM((2, cols // 4, 4, rows, LANES), F32),
             pltpu.VMEM((cols * rows, 2 * LANES), BF16),
             pltpu.VMEM((cols * rows, 2 * LANES), BF16),
@@ -406,13 +464,14 @@
             pltpu.VMEM(blocks, F32),
             pltpu.SemaphoreType.DMA,
             pltpu.SemaphoreType.DMA((2,)),
+            pltpu.SemaphoreType.DMA((5,)),
             pltpu.SemaphoreType.REGULAR((tms,)),
             pltpu.SemaphoreType.REGULAR,
             dma, dma, dma, dma,
         ],
         compiler_params=pltpu.CompilerParams(collective_id=0, has_side_effects=True),
         name="front",
-    )(signal, coarse_taps, index, tw_c, wh, wl)
+    )(signal, coarse_taps, channel_order, tw_c, wh, wl)
 
 
 def tables(width, fine):

time: 119 us -> 114 us (0.958)
  the two profiles are of different devices: /device:TPU:66 before, /device:TPU:192 now
where the time goes in v3:
time: 114 us
  Pallas kernels  112 us (98%)
  other arithmetic  1.37 us (1%)
    pallas_call x1, Pallas kernels, run_front(): pl.pallas_call(front_kernel, out_shape=jax.ShapeDtypeStruct(blocks, F32),...  106 us
    pallas_call x1, Pallas kernels, run_fine(): pl.pallas_call(fine_kernel, out_shape=jax.ShapeDtypeStruct((2, 1, own, fr...  5.75 us

profile of v3, /device:TPU:192, one launch (start us, length us, event | category | flops | bytes accessed | tf_op | source)
XLA Modules:
  0.0 114.1 jit_solution(13124200048570310446)
XLA Ops:
  0.0 0.0 copy-start
  0.0 1.4 %fusion.1.index_ref = s32[4096]{0:T(1024)} fusion(s32[4096]{0:T(1024)} %param.11), kind=kLoop, calls=%fused_computation.7 | loop fusion | flops 86016 | bytes 32768 | tf_op jit(solution)/shard_map/add | solution.py:509
  1.4 0.0 copy-done
  1.4 0.6 bitcast_bitcast_fusion.taps_ref
  2.0 106.3 %front.1 = f32[2,16,8,8,128]{4,3,2,1,0:T(8,128)} custom-call(f32[2,1,32,4096]{3,2,1,0:T(8,128)} %sig_ref.1, f32[16,4096]{1,0:T(8,128)} %taps_ref.1, s32[4096]{0:T(1024)} %fusion.1.index_ref, f32[2,32,128]{2,1,0:T(8,128)} %constant.40.clone.tw_ref, bf16[256,256]{1,0:T(8,128)(2,1)} %constant.38.clone.wh_ref, bf16[256,256]{1,0:T(8,128)(2,1)} %constant.39.clone.wl_ref), custom_call_target="tpu_custom_call" | custom-call | tf_op jit(solution)/shard_map/front/pallas_call | solution.py:447
  108.3 5.8 %fine.1 = f32[2,1,32,4,1024]{4,3,2,1,0:T(4,128)} custom-call(f32[2,128,8,128]{3,2,1,0:T(8,128)} %bitcast.8, f32[8,16,128]{2,1,0:T(8,128)} %bitcast_bitcast_fusion.taps_ref, f32[2,8,128]{2,1,0:T(8,128)} %constant.41.clone.tw_ref, bf16[256,256]{1,0:T(8,128)(2,1)} %constant.38.clone.wh_ref, bf16[256,256]{1,0:T(8,128)(2,1)} %constant.39.clone.wl_ref), custom_call_target="tpu_custom_call" | custom-call | tf_op jit(solution)/shard_map/fine/pallas_call | solution.py:487
Async XLA Ops:
  0.0 1.4 %copy-start = (f32[16,1024]{1,0:T(8,128)S(1)}, f32[16,1024]{1,0:T(8,128)}, u32[]{:S(2)}) copy-start(f32[16,1024]{1,0:T(8,128)} %param.10) | copy-start | bytes 196612

commit v4 on v3

--- a/solution.py
+++ b/solution.py
@@ -225,7 +225,7 @@
     fine_fft(xs_scr, tw_ref, wh_ref, wl_ref, p_scr, out_ref)
 
 
-EARLY = 5
+EARLY = 4
 
 
 def front_kernel(sig_ref, taps_ref, index_ref, tw_ref, wh_ref, wl_ref, arr_ref,
@@ -282,6 +282,15 @@
         return pltpu.make_async_remote_copy(
             source, second, leg_sem.at[2], leg_sem.at[3], device_id={"tm": z - 1}, device_id_type=mesh_id)
 
+    def first_down():
+        down(sig_ref.at[:, 0, pl.ds(0, lead), pl.ds(0, piece)]).start()
+
+    def hand_down():
+        @pl.when(inner)
+        def _():
+            wait_for(first, leg_sem.at[1])
+            down(first).start()
+
     def to_edge():
         return pltpu.make_async_remote_copy(
             second, halo.at[:, :, pl.ds(pl.multiple_of(x * piece, piece), piece)],
@@ -306,6 +315,13 @@
             blk.at[half, j], relay.at[half, z], far_send.at[half, j], far_recv.at[half, z],
             device_id={"tm": j}, device_id_type=mesh_id).start()
 
+    def hear(j):
+        pl.semaphore_wait(in_sem.at[j], 1)
+
+        @pl.when(z == 1)
+        def _():
+            tell(in_sem.at[j], tm=0)
+
     def half_step(half):
         @pl.when(half == 0)
         def _():
@@ -321,18 +337,22 @@
             def _():
                 halo_copy().start()
 
-            @pl.when(lower)
-            def _():
-                pl.semaphore_wait(below, 1)
-
-            @pl.when(z < last)
-            def _():
-                tell(below, tm=z + 1)
-                loop(0, z, lambda j: tell(in_sem.at[z + 1], tm=j))
-
-            @pl.when(both(x == 0, lower))
-            def _():
-                down(sig_ref.at[:, 0, pl.ds(0, lead), pl.ds(0, piece)]).start()
+            @pl.when(z > 1)
+            def _():
+                pl.semaphore_wait(below.at[0], 1)
+
+            @pl.when(z == 0)
+            def _():
+                tell(below.at[1], tm=z + 1)
+
+            @pl.when(both(lower, upper))
+            def _():
+                tell(below.at[0], tm=z + 1)
+                loop(1, z, lambda j: tell(in_sem.at[z + 1], tm=j))
+
+            @pl.when(both(x == 0, z > 1))
+            def _():
+                first_down()
 
         @pl.when(half == 1)
         def _():
@@ -358,29 +378,53 @@
 
         coarse_fft(half, rows, x_scr, taps_ref, tw_ref, wh_ref, wl_ref, u_scr, lh_scr, ll_scr, y_scr)
 
+        @pl.when(both(half == 1, both(middle, upper)))
+        def _():
+            wait_for(second, leg_sem.at[3])
+            to_edge().start()
+
         def put(q, r, vec):
             owner = 4 * q + r
             blk[half, owner // sects, owner % sects] = vec
 
         order_channels(index_ref, y_scr, z_scr, g_scr, put)
 
-        @pl.when(both(half == 0, both(inner, lower)))
-        def _():
-            wait_for(first, leg_sem.at[1])
-            down(first).start()
-
-        @pl.when(both(half == 1, both(middle, upper)))
-        def _():
-            wait_for(second, leg_sem.at[3])
-            to_edge().start()
-
-        loop(0, z, lambda j: across(half, j))
+        @pl.when(both(half == 0, z > 1))
+        def _():
+            hand_down()
+
+        @pl.when(both(half == 1, lower))
+        def _():
+            across(half, 0)
+
+        loop(1, z, lambda j: across(half, j))
         spread(blk.at[half, z], half, z)
+
+        @pl.when(both(half == 0, lower))
+        def _():
+            pl.semaphore_wait(below.at[1], 1)
+
+            @pl.when(upper)
+            def _():
+                tell(below.at[1], tm=z + 1)
+
+            @pl.when(z == 1)
+            def _():
+                tell(in_sem.at[z + 1], tm=0)
+                hand_down()
+
+                @pl.when(x == 0)
+                def _():
+                    first_down()
+
+        @pl.when(both(half == 0, lower))
+        def _():
+            across(half, 0)
 
         def early(s):
             @pl.when(jnp.logical_and(half == 0, s > 0))
             def _():
-                pl.semaphore_wait(in_sem.at[z + 1 + s], 1)
+                hear(z + 1 + s)
 
             across(half, z + 1 + s)
 
@@ -390,7 +434,7 @@
     loop(0, 2, half_step)
 
     def later(s):
-        pl.semaphore_wait(in_sem.at[z + 1 + s], 1)
+        hear(z + 1 + s)
         for half in range(2):
             across(half, z + 1 + s)
 
@@ -466,7 +510,7 @@
             pltpu.SemaphoreType.DMA((2,)),
             pltpu.SemaphoreType.DMA((5,)),
             pltpu.SemaphoreType.REGULAR((tms,)),
-            pltpu.SemaphoreType.REGULAR,
+            pltpu.SemaphoreType.REGULAR((2,)),
             dma, dma, dma, dma,
         ],
         compiler_params=pltpu.CompilerParams(collective_id=0, has_side_effects=True),

time: 114 us -> 107 us (0.939)
  the two profiles are of different devices: /device:TPU:192 before, /device:TPU:66 now
where the time goes in v4:
time: 107 us; the launch traced here: 106 us
  Pallas kernels  104 us (97%)
  other arithmetic  1.37 us (1%)
    pallas_call x1, Pallas kernels, run_front(): pl.pallas_call(front_kernel, out_shape=jax.ShapeDtypeStruct(blocks, F32),...  98.5 us
    pallas_call x1, Pallas kernels, run_fine(): pl.pallas_call(fine_kernel, out_shape=jax.ShapeDtypeStruct((2, 1, own, fr...  5.75 us

profile of v4, /device:TPU:66, one launch (start us, length us, event | category | flops | bytes accessed | tf_op | source)
XLA Modules:
  0.0 106.3 jit_solution(2274519085815167689)
XLA Ops:
  0.0 0.0 copy-start
  0.0 1.4 %fusion.1.index_ref = s32[4096]{0:T(1024)} fusion(s32[4096]{0:T(1024)} %param.11), kind=kLoop, calls=%fused_computation.7 | loop fusion | flops 86016 | bytes 32768 | tf_op jit(solution)/shard_map/add | solution.py:553
  1.4 0.0 copy-done
  1.4 0.6 bitcast_bitcast_fusion.taps_ref
  2.0 98.5 %front.1 = f32[2,16,8,8,128]{4,3,2,1,0:T(8,128)} custom-call(f32[2,1,32,4096]{3,2,1,0:T(8,128)} %sig_ref.1, f32[16,4096]{1,0:T(8,128)} %taps_ref.1, s32[4096]{0:T(1024)} %fusion.1.index_ref, f32[2,32,128]{2,1,0:T(8,128)} %constant.40.clone.tw_ref, bf16[256,256]{1,0:T(8,128)(2,1)} %constant.38.clone.wh_ref, bf16[256,256]{1,0:T(8,128)(2,1)} %constant.39.clone.wl_ref), custom_call_target="tpu_custom_call" | custom-call | tf_op jit(solution)/shard_map/front/pallas_call | solution.py:491
  100.5 5.8 %fine.1 = f32[2,1,32,4,1024]{4,3,2,1,0:T(4,128)} custom-call(f32[2,128,8,128]{3,2,1,0:T(8,128)} %bitcast.8, f32[8,16,128]{2,1,0:T(8,128)} %bitcast_bitcast_fusion.taps_ref, f32[2,8,128]{2,1,0:T(8,128)} %constant.41.clone.tw_ref, bf16[256,256]{1,0:T(8,128)(2,1)} %constant.38.clone.wh_ref, bf16[256,256]{1,0:T(8,128)(2,1)} %constant.39.clone.wl_ref), custom_call_target="tpu_custom_call" | custom-call | tf_op jit(solution)/shard_map/fine/pallas_call | solution.py:531
Async XLA Ops:
  0.0 1.4 %copy-start = (f32[16,1024]{1,0:T(8,128)S(1)}, f32[16,1024]{1,0:T(8,128)}, u32[]{:S(2)}) copy-start(f32[16,1024]{1,0:T(8,128)} %param.10) | copy-start | bytes 196612

commit v5 on v4

--- a/solution.py
+++ b/solution.py
@@ -75,16 +75,25 @@
 
 def group_transpose(vecs, lane):
     size = LANES // 4
-    vecs = list(vecs)
-    for dist in (1, 2):
-        keep = (lane // (size * dist)) % 2 == 0
-        for i in range(4):
-            if i & dist:
-                continue
-            a, b = vecs[i], vecs[i + dist]
-            vecs[i] = jnp.where(keep, a, pltpu.roll(b, size * dist, 1))
-            vecs[i + dist] = jnp.where(keep, pltpu.roll(a, LANES - size * dist, 1), b)
-    return vecs
+    group = lane // size
+    odd, high = group % 2 == 1, group >= 2
+    outer = (group == 0) | (group == 3)
+
+    def pair(a, b):
+        turned = pltpu.roll(jnp.where(odd, a, b), size, 1)
+        return jnp.where(odd, turned, a), jnp.where(odd, b, turned)
+
+    a, b = pair(vecs[0], vecs[1])
+    c, d = pair(vecs[2], vecs[3])
+    even = pltpu.roll(jnp.where(high, a, c), 2 * size, 1)
+    rest = pltpu.roll(jnp.where(high, b, d), 2 * size, 1)
+    kept = jnp.where(high, d, b)
+    return [
+        jnp.where(high, even, a),
+        jnp.where(outer, rest, kept),
+        jnp.where(high, c, even),
+        jnp.where(outer, kept, rest),
+    ]
 
 
 def coarse_fft(half, rows, x_scr, taps_ref, tw_ref, wh_ref, wl_ref, u_scr, lh_scr, ll_scr, y_scr):
@@ -136,11 +145,13 @@
     row_lane = lax.broadcasted_iota(jnp.int32, (1, LANES), 1)
     group = LANES // 4
     chunk = 16
-
-    def step(part, carry):
+    runs, batch = LANES // chunk, g_scr.shape[0]
+
+    def step(quad, carry):
         def fetch(i, inner):
-            lists = [index_ref.at[pl.ds((part * 4 + h) * LANES + i * chunk, chunk)] for h in range(4)]
-            spot = g_scr.at[pl.ds(pl.multiple_of(i * chunk, chunk), chunk), :]
+            part, row = quad * batch + i // runs, i % runs * chunk
+            lists = [index_ref.at[pl.ds((part * 4 + h) * LANES + row, chunk)] for h in range(4)]
+            spot = g_scr.at[i // runs, pl.ds(pl.multiple_of(row, chunk), chunk), :]
             for u in range(chunk):
                 got = [z_scr[pl.ds(lists[h][u], 1), :] for h in range(4)]
                 low = jnp.where(row_lane < group, got[0], got[1])
@@ -148,15 +159,16 @@
                 spot[u : u + 1, :] = jnp.where(row_lane < 2 * group, low, high)
             return inner
 
-        lax.fori_loop(0, LANES // chunk, fetch, 0)
-        turned = jnp.transpose(g_scr[...])
-        for h in range(4):
-            vecs = [turned[(h * 4 + u) * SUB : (h * 4 + u + 1) * SUB] for u in range(4)]
-            for r, vec in enumerate(group_transpose(vecs, lane)):
-                put(part * 4 + h, r, vec)
+        lax.fori_loop(0, batch * runs, fetch, 0)
+        for p in range(batch):
+            turned = jnp.transpose(g_scr[p])
+            for h in range(4):
+                vecs = [turned[(h * 4 + u) * SUB : (h * 4 + u + 1) * SUB] for u in range(4)]
+                for r, vec in enumerate(group_transpose(vecs, lane)):
+                    put((quad * batch + p) * 4 + h, r, vec)
         return carry
 
-    lax.fori_loop(0, cols // 4, step, 0)
+    lax.fori_loop(0, cols // 4 // batch, step, 0)
 
 
 def fine_fir(arr_ref, taps_ref, xs_scr, frames, per):
@@ -190,7 +202,7 @@
                     xs_scr[u // 2, pl.ds(base, SUB), :] = vec
         return carry
 
-    lax.fori_loop(0, per // 4, step, 0)
+    lax.fori_loop(0, per // 4, step, 0, unroll=2)
 
 
 def fine_fft(xs_scr, tw_ref, wh_ref, wl_ref, p_scr, out_ref):
@@ -503,7 +515,7 @@
             pltpu.VMEM((cols * rows, 2 * LANES), BF16),
             pltpu.VMEM((2, cols, rows, LANES), F32),
             pltpu.VMEM((width, LANES), F32),
-            pltpu.VMEM((LANES, LANES), F32),
+            pltpu.VMEM((4, LANES, LANES), F32),
             pltpu.VMEM(blocks, F32),
             pltpu.VMEM(blocks, F32),
             pltpu.SemaphoreType.DMA,

time: 107 us -> 104 us (0.972)
  the two profiles are of different devices: /device:TPU:66 before, /device:TPU:192 now
where the time goes in v5:
time: 104 us
  Pallas kernels  102 us (98%)
  other arithmetic  1.37 us (1%)
    pallas_call x1, Pallas kernels, run_front(): pl.pallas_call(front_kernel, out_shape=jax.ShapeDtypeStruct(blocks, F32),...  96.8 us
    pallas_call x1, Pallas kernels, run_fine(): pl.pallas_call(fine_kernel, out_shape=jax.ShapeDtypeStruct((2, 1, own, fr...  4.93 us

profile of v5, /device:TPU:192, one launch (start us, length us, event | category | flops | bytes accessed | tf_op | source)
XLA Modules:
  0.0 103.7 jit_solution(5103761168257168251)
XLA Ops:
  0.0 0.0 copy-start
  0.0 1.4 %fusion.1.index_ref = s32[4096]{0:T(1024)} fusion(s32[4096]{0:T(1024)} %param.11), kind=kLoop, calls=%fused_computation.7 | loop fusion | flops 86016 | bytes 32768 | tf_op jit(solution)/shard_map/add | solution.py:565
  1.4 0.0 copy-done
  1.4 0.6 bitcast_bitcast_fusion.taps_ref
  2.0 96.8 %front.1 = f32[2,16,8,8,128]{4,3,2,1,0:T(8,128)} custom-call(f32[2,1,32,4096]{3,2,1,0:T(8,128)} %sig_ref.1, f32[16,4096]{1,0:T(8,128)} %taps_ref.1, s32[4096]{0:T(1024)} %fusion.1.index_ref, f32[2,32,128]{2,1,0:T(8,128)} %constant.40.clone.tw_ref, bf16[256,256]{1,0:T(8,128)(2,1)} %constant.38.clone.wh_ref, bf16[256,256]{1,0:T(8,128)(2,1)} %constant.39.clone.wl_ref), custom_call_target="tpu_custom_call" | custom-call | tf_op jit(solution)/shard_map/front/pallas_call | solution.py:503
  98.8 4.9 %fine.1 = f32[2,1,32,4,1024]{4,3,2,1,0:T(4,128)} custom-call(f32[2,128,8,128]{3,2,1,0:T(8,128)} %bitcast.8, f32[8,16,128]{2,1,0:T(8,128)} %bitcast_bitcast_fusion.taps_ref, f32[2,8,128]{2,1,0:T(8,128)} %constant.41.clone.tw_ref, bf16[256,256]{1,0:T(8,128)(2,1)} %constant.38.clone.wh_ref, bf16[256,256]{1,0:T(8,128)(2,1)} %constant.39.clone.wl_ref), custom_call_target="tpu_custom_call" | custom-call | tf_op jit(solution)/shard_map/fine/pallas_call | solution.py:543
Async XLA Ops:
  0.0 1.4 %copy-start = (f32[16,1024]{1,0:T(8,128)S(1)}, f32[16,1024]{1,0:T(8,128)}, u32[]{:S(2)}) copy-start(f32[16,1024]{1,0:T(8,128)} %param.10) | copy-start | bytes 196612

commit v6 on v5

--- a/solution.py
+++ b/solution.py
@@ -202,7 +202,7 @@
                     xs_scr[u // 2, pl.ds(base, SUB), :] = vec
         return carry
 
-    lax.fori_loop(0, per // 4, step, 0, unroll=2)
+    lax.fori_loop(0, per // 4, step, 0, unroll=4)
 
 
 def fine_fft(xs_scr, tw_ref, wh_ref, wl_ref, p_scr, out_ref):
@@ -228,7 +228,7 @@
                     comp].reshape(pack, frames, LANES)
         return carry
 
-    lax.fori_loop(0, LANES // SUB, step, 0)
+    lax.fori_loop(0, LANES // SUB, step, 0, unroll=2)
 
 
 def fine_kernel(arr_ref, taps_ref, tw_ref, wh_ref, wl_ref, out_ref, xs_scr, p_scr):

time: 104 us -> 106 us (1.019)
  Pallas kernels: 102 us -> 104 us
    pallas_call x1, Pallas kernels: 4.93 us -> 6.85 us  [run_fine(): pl.pallas_call(fine_kernel, out_shape=jax.ShapeDtypeStruct((2, 1, own, fr...]
where the time goes in v6:
time: 106 us
  Pallas kernels  104 us (98%)
  other arithmetic  1.37 us (1%)
    pallas_call x1, Pallas kernels, run_front(): pl.pallas_call(front_kernel, out_shape=jax.ShapeDtypeStruct(blocks, F32),...  96.8 us
    pallas_call x1, Pallas kernels, run_fine(): pl.pallas_call(fine_kernel, out_shape=jax.ShapeDtypeStruct((2, 1, own, fr...  6.85 us

profile of v6, /device:TPU:192, one launch (start us, length us, event | category | flops | bytes accessed | tf_op | source)
XLA Modules:
  0.0 105.7 jit_solution(1037410767839802853)
XLA Ops:
  0.0 0.0 copy-start
  0.0 1.4 %fusion.1.index_ref = s32[4096]{0:T(1024)} fusion(s32[4096]{0:T(1024)} %param.11), kind=kLoop, calls=%fused_computation.7 | loop fusion | flops 86016 | bytes 32768 | tf_op jit(solution)/shard_map/add | solution.py:565
  1.4 0.0 copy-done
  1.4 0.6 bitcast_bitcast_fusion.taps_ref
  2.0 96.8 %front.1 = f32[2,16,8,8,128]{4,3,2,1,0:T(8,128)} custom-call(f32[2,1,32,4096]{3,2,1,0:T(8,128)} %sig_ref.1, f32[16,4096]{1,0:T(8,128)} %taps_ref.1, s32[4096]{0:T(1024)} %fusion.1.index_ref, f32[2,32,128]{2,1,0:T(8,128)} %constant.40.clone.tw_ref, bf16[256,256]{1,0:T(8,128)(2,1)} %constant.38.clone.wh_ref, bf16[256,256]{1,0:T(8,128)(2,1)} %constant.39.clone.wl_ref), custom_call_target="tpu_custom_call" | custom-call | tf_op jit(solution)/shard_map/front/pallas_call | solution.py:503
  98.8 6.8 %fine.1 = f32[2,1,32,4,1024]{4,3,2,1,0:T(4,128)} custom-call(f32[2,128,8,128]{3,2,1,0:T(8,128)} %bitcast.8, f32[8,16,128]{2,1,0:T(8,128)} %bitcast_bitcast_fusion.taps_ref, f32[2,8,128]{2,1,0:T(8,128)} %constant.41.clone.tw_ref, bf16[256,256]{1,0:T(8,128)(2,1)} %constant.38.clone.wh_ref, bf16[256,256]{1,0:T(8,128)(2,1)} %constant.39.clone.wl_ref), custom_call_target="tpu_custom_call" | custom-call | tf_op jit(solution)/shard_map/fine/pallas_call | solution.py:543
Async XLA Ops:
  0.0 1.4 %copy-start = (f32[16,1024]{1,0:T(8,128)S(1)}, f32[16,1024]{1,0:T(8,128)}, u32[]{:S(2)}) copy-start(f32[16,1024]{1,0:T(8,128)} %param.10) | copy-start | bytes 196612
